TPU v7x, 128 devices: a whole 4x4x4 slice. The times are simulated.
128 devices in a mesh: teacher: 8 (over z_hi, y), student: 16 (over z_lo, x, core).
Axes of the slice: x: 4, y: 4, z: 4 (z_hi: 2, z_lo: 2; z = z_hi * 2 + z_lo), core: 2. Of those that a mesh axis runs over, the one named last changes fastest.
Arguments:
- teacher_in: bfloat16 [16384, 8192], P('student', 'teacher')
- teacher_attn: bfloat16 [16384, 4096], P('student', 'teacher'), may hold values from -6 to 6
- teacher_out_proj: bfloat16 [4096, 8192], P('student', 'teacher'), may hold values from -0.09375 to 0.09375
- teacher_gain: bfloat16 [8192], P('teacher'), may hold values from 0.099609375 to 1.8984375
- projection: bfloat16 [8192, 4096], P('teacher', 'student'), may hold values from -0.0625 to 0.0625
- student_in: bfloat16 [16384, 4096], P('student', 'teacher')
- student_attn: bfloat16 [16384, 2048], P('student', 'teacher'), may hold values from -6 to 6
- student_out_proj: bfloat16 [2048, 4096], P('student', 'teacher'), may hold values from -0.125 to 0.125
- student_gain: bfloat16 [4096], P('teacher'), may hold values from 0.099609375 to 1.8984375
- token_ids: int32 [16384], P('student'), may hold values from 0 to 128004, as said below
- row_order: int32 [16384], replicated, may hold values from 0 to 16383, as said below
Outputs:
- grad_weight: float32 [2048, 4096], P('student', 'teacher')
- grad_gain: float32 [4096], P('teacher')
Inputs may be any that keep to these rules, and one draw needn't show every extreme that they name: `token_ids`: within each sequence of 1024 consecutive rows the rows holding 128004 form the sequence's tail, after at least 256 other rows; no other row holds 128004. `row_order`: A permutation of the 16384 rows. For student block k and teacher block b (blocks of 1024 rows), the entries k * 1024 + b * 64 to k * 1024 + (b + 1) * 64 - 1 name rows of teacher block b.
All inputs are finite; a program needn't handle non-finite values.
Results may differ from a plain program's by a relative error of at most 0.02.
Values may be sent and summed in bfloat16 or wider, within the bound.
A program may use at most 128 MiB of HBM per device.

v0:
```python
import math
import jax
import jax.numpy as jnp
from jax import lax
from jax.sharding import PartitionSpec as P

DT = 8192
DS = 4096
PAD_ID = 128004
epsilon = 1e-05


def rows_first(arrays, axis, dims):
    turned = [jnp.moveaxis(a, dim, 0) for a, dim in zip(arrays, dims)]
    both = jnp.concatenate([t.reshape(len(t), -1) for t in turned], axis=1)
    result, at, outs = (lax.all_gather(both, axis, axis=0, tiled=True), 0, [])
    for t, dim in zip(turned, dims):
        section = result[:, at : at + t[0].size].reshape(-1, *t.shape[1:])
        outs.append(jnp.moveaxis(section, 0, dim))
        at += t[0].size
    return tuple(outs)


def sent_to_all(array, axis):
    peers = lax.axis_size(axis)
    return lax.all_to_all(
        jnp.broadcast_to(array[None], (peers, *array.shape)), axis, 0, 0, tiled=True
    )


def of_everyone(array, axis):
    everything = sent_to_all(array, axis)
    return jnp.sum(everything, axis=0)


def sent_together(arrays, axis, split_dim, concat_dim, along):
    columns = [a.reshape(*a.shape[:along], -1) for a in arrays]
    both = jnp.concatenate(columns, axis=along)
    result, at, outs = (
        lax.all_to_all(both, axis, split_axis=split_dim, concat_axis=concat_dim, tiled=True),
        0,
        [],
    )
    for a, column in zip(arrays, columns):
        section = result[..., at : at + column.shape[along]]
        outs.append(section.reshape(*section.shape[:along], *a.shape[along:]))
        at += column.shape[along]
    return tuple(outs)


def in_blocks(array, dim, peers):
    shape = array.shape
    parts = array.reshape(*shape[:dim], peers, shape[dim] // peers, *shape[dim + 1 :])
    return jnp.moveaxis(parts, dim, 0)


def sent_and_summed(array, axis, dim):
    peers = lax.axis_size(axis)
    parts = lax.all_to_all(in_blocks(array, dim, peers), axis, 0, 0, tiled=True)
    return jnp.sum(parts.astype(jnp.float32), axis=0)


def shards(
    teacher_in,
    teacher_attn,
    teacher_out_proj,
    teacher_gain,
    projection,
    student_in,
    student_attn,
    student_out_proj,
    student_gain,
    token_ids,
    row_order,
):
    student_count = lax.axis_size("student")
    teacher_count = lax.axis_size("teacher")
    row_count = teacher_in.shape[0]
    piece_rows = row_count // student_count
    student_index = lax.axis_index("student")
    attn_all = lax.all_gather(teacher_attn, "teacher", axis=1, tiled=True)
    out_full, proj_full = rows_first((teacher_out_proj, projection), "student", (0, 1))
    branch = jnp.dot(attn_all, out_full, preferred_element_type=jnp.float32)
    residual = teacher_in.astype(jnp.float32) + branch
    square_sum = of_everyone(jnp.sum(residual * residual, axis=1), "teacher")
    teacher_scale = lax.rsqrt(square_sum / DT + epsilon)
    hidden = (residual * teacher_scale[:, None] * teacher_gain.astype(jnp.float32)[None, :]).astype(
        jnp.bfloat16
    )
    proj_blocks = proj_full.reshape(
        proj_full.shape[0], teacher_count, proj_full.shape[1] // teacher_count
    )
    row_blocks = row_order.reshape(student_count, student_count, piece_rows)
    local_rows = (
        lax.dynamic_index_in_dim(row_blocks, student_index, 1, keepdims=False)
        - student_index * row_count
    )
    live_rows = jnp.where(token_ids != PAD_ID, 1.0, 0.0).astype(jnp.bfloat16)
    mask_send = jnp.take(live_rows, local_rows, axis=0)
    columns = proj_blocks
    summed = lax.psum_scatter(
        jnp.einsum("tf,fko->kto", hidden, columns, preferred_element_type=jnp.float32).astype(
            jnp.bfloat16
        ),
        "teacher",
        scatter_dimension=0,
        tiled=True,
    ).astype(jnp.float32)
    target_rows = summed[0].astype(jnp.bfloat16)
    moved, mask_got = sent_together(
        (jnp.take(target_rows, local_rows, axis=0), mask_send), "student", 0, 0, 2
    )
    target = moved.reshape(row_count, moved.shape[2])
    weight_mask = mask_got.reshape(row_count).astype(jnp.float32)
    attn_student = lax.all_gather(student_attn, "teacher", axis=1, tiled=True)
    columns = attn_student
    student_branch = jnp.dot(
        columns,
        lax.all_gather(student_out_proj, "student", axis=0, tiled=True),
        preferred_element_type=jnp.float32,
    )
    student_res = student_in.astype(jnp.float32) + student_branch
    student_square = of_everyone(jnp.sum(student_res * student_res, axis=1), "teacher")
    student_scale = lax.rsqrt(student_square / DS + epsilon)
    normed = student_res * student_scale[:, None]
    gain_values = student_gain.astype(jnp.float32)[None, :]
    distance = normed * gain_values - target.astype(jnp.float32)
    loss_weight = 1.0 / math.sqrt(row_count * student_count)
    grad_out = distance * (weight_mask * loss_weight)[:, None]
    gain_part = jnp.sum(grad_out * normed, axis=0)
    grad_norm = grad_out * gain_values
    inner_sum = of_everyone(jnp.sum(grad_norm * normed, axis=1), "teacher")
    grad_res = (student_scale[:, None] * (grad_norm - normed * (inner_sum / DS)[:, None])).astype(
        jnp.bfloat16
    )
    columns = attn_student
    grad_weight = sent_and_summed(
        lax.dot_general(
            columns, grad_res, (((0,), (0,)), ((), ())), preferred_element_type=jnp.float32
        ).astype(jnp.bfloat16),
        "student",
        0,
    )
    grad_gain = of_everyone(gain_part, "student")
    return (grad_weight, grad_gain)


def solution(mesh):
    placed = (
        P("student", "teacher"),
        P("student", "teacher"),
        P("student", "teacher"),
        P("teacher"),
        P("teacher", "student"),
        P("student", "teacher"),
        P("student", "teacher"),
        P("student", "teacher"),
        P("teacher"),
        P("student"),
        P(),
    )
    return jax.shard_map(
        shards,
        mesh=mesh,
        in_specs=placed,
        out_specs=(P("student", "teacher"), P("teacher")),
        check_vma=False,
    )
```

profile of v0, /device:TPU:3, one launch (start us, length us, event | category | flops | bytes accessed | tf_op | source)
XLA Modules:
  0.0 564.8 jit_solution(5684495137640013331)
XLA Ops:
  7.2 0.7 all-gather.11.cloned.1.call-update
  8.0 1.2 copy.60
  9.2 1.1 pad_maximum_fusion.1
  10.4 0.7 all-gather.7.cloned.1.call-update
  11.1 0.5 all-gather.5.cloned.1.call-update
  11.7 2.6 copy.62
  14.3 116.5 %all-gather.11.cloned.1.call-done = bf16[1024,4096]{1,0:T(8,128)(2,1)} async-done(((bf16[1024,512]{1,0:T(8,128)(2,1)}), bf16[1024,4096]{1,0:T(8,128)(2,1)}) %all-gather.11.cloned.1.call-update) | async-done | bytes 8388624 | tf_op jit(solution)/shard_map/all_gather | solution.py:81
  130.8 99.5 %all-gather.9.cloned.1.call-done = bf16[4096,2048]{0,1:T(8,128)(2,1)} async-done(((bf16[256,2048]{0,1:T(8,128)(2,1)}), bf16[4096,2048]{0,1:T(8,128)(2,1)}) %all-gather.9.cloned.1.call-update) | async-done | bytes 16777232 | tf_op jit(solution)/shard_map/all_gather | solution.py:16
  230.3 15.4 %multiply_reduce_fusion = (f32[1024]{0:T(1024)S(1)}, f32[1024,1024]{1,0:T(8,128)}) fusion(bf16[1024,1024]{0,1:T(8,128)(2,1)} %copy.62, bf16[1024,4096]{1,0:T(8,128)(2,1)} %all-gather.11.cloned.1.call-done, bf16[4096,2048]{0,1:T(8,128)(2,1)} %all-gather.9.cloned.1.call-done), kind=kOutput, calls=%fused_computation.9 | convolution fusion | flops 8594127872 | bytes 23072768 | tf_op jit(solution)/shard_map/dot_general | solution.py:83
  245.8 0.6 broadcast_in_dim.34
  246.4 6.3 %all-to-all-start.1 = ((f32[8,1,1024]{2,1,0:T(1,128)}), f32[8,1,1024]{2,1,0:T(1,128)S(1)}, u32[]{:S(2)}, u32[]{:S(2)}) async-start(f32[8,1,1024]{2,1,0:T(1,128)} %broadcast_in_dim.34), calls=%async_computation.1 | async-start | bytes 65536 | tf_op jit(solution)/shard_map/all_to_all | solution.py:26
  252.7 0.2 reduce-scatter.2.cloned.1.call-start
  252.9 7.8 %slice_bitcast_fusion = bf16[1024,4096]{1,0:T(8,128)(2,1)} fusion(bf16[4096,2048]{0,1:T(8,128)(2,1)} %all-gather.9.cloned.1.call-done), kind=kLoop, calls=%fused_computation.4 | loop fusion | bytes 16777216 | tf_op jit(solution)/shard_map/transpose | solution.py:19
  260.7 12.1 %copy.61 = bf16[1024,4096]{0,1:T(8,128)(2,1)} copy(bf16[1024,4096]{1,0:T(8,128)(2,1)} %slice_bitcast_fusion) | data formatting | bytes 16777216 | tf_op jit(solution)/shard_map/transpose | solution.py:19
  272.9 15.4 %convert_bitcast_fusion = bf16[8,1024,512]{1,2,0:T(8,128)(2,1)} fusion(bf16[1024,8,512]{0,2,1:T(8,128)(2,1)} %bitcast.38, f32[1024,1024]{1,0:T(8,128)} %get-tuple-element.11, bf16[1024,1024]{0,1:T(8,128)(2,1)S(1)} %copy-done.1, f32[1024]{0:T(1024)S(1)} %convert_element_type.58, f32[1024]{0:T(1024)S(1)} %add_rsqrt_fusion), kind=kOutput, calls=%fused_computation.5 | convolution fusion | flops 8599371776 | bytes 23076864 | tf_op jit(solution)/shard_map/tf,fko->kto/dot_general | solution.py:102
  288.4 0.8 copy-done.4
  289.2 0.1 reshape.115
  289.4 6.8 %gather_fusion.1 = bf16[1024]{0:T(1024)(128)(2,1)S(1)} fusion(bf16[1024]{0:T(1024)(128)(2,1)S(1)} %select_convert_fusion, s32[1024]{0:T(1024)S(1)} %broadcast_clamp_fusion), kind=kCustom, calls=%fused_computation.1 | custom fusion | bytes 8192 | tf_op jit(solution)/shard_map/jit(_take)/gather | solution.py:99
  296.2 0.1 gather.12
  296.3 0.2 copy.66
  296.6 0.5 copy.58
  297.1 46.7 %all-gather.5.cloned.1.call-done = bf16[1024,2048]{1,0:T(8,128)(2,1)} async-done(((bf16[1024,256]{1,0:T(8,128)(2,1)}), bf16[1024,2048]{1,0:T(8,128)(2,1)}) %all-gather.5.cloned.1.call-update) | async-done | bytes 4194320 | tf_op jit(solution)/shard_map/all_gather | solution.py:115
  343.9 6.6 %multiply_reduce_fusion.3 = (f32[1024]{0:T(1024)S(1)}, f32[1024,512]{0,1:T(8,128)}) fusion(bf16[1024,2048]{1,0:T(8,128)(2,1)} %all-gather.5.cloned.1.call-done, bf16[2048,512]{1,0:T(8,128)(2,1)} %all-gather.7.cloned.1.call-done, bf16[1024,512]{0,1:T(8,128)(2,1)S(1)} %copy.58), kind=kOutput, calls=%fused_computation.19 | convolution fusion | flops 2149579776 | bytes 9441280 | tf_op jit(solution)/shard_map/dot_general | solution.py:117
  350.5 0.6 broadcast_in_dim.32
  351.1 3.4 all-to-all-start
  354.5 107.1 %reduce-scatter.2.cloned.1.call-done = bf16[1,1024,512]{1,2,0:T(8,128)(2,1)} async-done(((bf16[8,1024,512]{1,2,0:T(8,128)(2,1)}), bf16[1,1024,512]{1,2,0:T(8,128)(2,1)}) %reduce-scatter.2.cloned.1.call-update) | async-done | bytes 1048592 | tf_op jit(solution)/shard_map/reduce_scatter | solution.py:101
  461.6 1.5 copy.65
  463.1 4.0 gather_fusion
  467.0 0.2 broadcast_select_fusion
  467.3 1.2 pad_maximum_fusion
  468.4 5.9 %all-to-all-start.2 = ((bf16[16,64,513]{2,1,0:T(8,128)(2,1)}), bf16[16,64,513]{2,1,0:T(8,128)(2,1)S(1)}, u32[]{:S(2)}, u32[]{:S(2)}) async-start(bf16[16,64,513]{2,1,0:T(8,128)(2,1)} %pad_maximum_fusion), calls=%async_computation.3 | async-start | bytes 2621440 | tf_op jit(solution)/shard_map/all_to_all | solution.py:40
  474.5 16.8 %all-to-all-done.2 = bf16[16,64,513]{2,1,0:T(8,128)(2,1)S(1)} async-done(((bf16[16,64,513]{2,1,0:T(8,128)(2,1)}), bf16[16,64,513]{2,1,0:T(8,128)(2,1)S(1)}, u32[]{:S(2)}, u32[]{:S(2)}) %all-to-all-start.2) | async-done | bytes 1050656 | tf_op jit(solution)/shard_map/all_to_all | solution.py:40
  491.2 0.1 slice.22
  491.3 1.7 bitcast_convert_fusion
  493.0 1.9 copy.67
  494.9 0.2 multiply_reduce_fusion.4
  495.2 0.1 mul.101
  495.2 2.4 multiply_reduce_fusion.1
  497.6 10.2 %all_to_all.34 = f32[8,1,1024]{2,1,0:T(1,128)S(1)} all-to-all(f32[8,1,1024]{2,1,0:T(1,128)S(1)} %broadcast_in_dim.62), channel_id=1, replica_groups=mesh['teacher'=8,'student'=16] {'teacher'}, dimensions={0} | all-to-all | bytes 65536 | tf_op jit(solution)/shard_map/all_to_all | solution.py:26
  507.8 0.6 broadcast_in_dim.63
  508.4 7.2 %all-to-all-start.5 = ((f32[16,1,512]{2,1,0:T(1,128)}), f32[16,1,512]{2,1,0:T(1,128)S(1)}, u32[]{:S(2)}, u32[]{:S(2)}) async-start(f32[16,1,512]{2,1,0:T(1,128)} %broadcast_in_dim.63), calls=%async_computation.6 | async-start | bytes 65536 | tf_op jit(solution)/shard_map/all_to_all | solution.py:26
  515.7 5.4 fusion.6
  521.1 1.9 copy.82
  523.0 5.8 %all-to-all-start.4 = ((bf16[16,128,512]{1,2,0:T(8,128)(2,1)}), bf16[16,128,512]{1,2,0:T(8,128)(2,1)S(1)}, u32[]{:S(2)}, u32[]{:S(2)}) async-start(bf16[16,128,512]{1,2,0:T(8,128)(2,1)} %bitcast.37), calls=%async_computation.5 | async-start | bytes 4194304 | tf_op jit(solution)/shard_map/all_to_all | solution.py:59
  528.8 0.6 reduce_sum.89
  529.4 27.7 %all-to-all-done.4 = bf16[16,128,512]{1,2,0:T(8,128)(2,1)S(1)} async-done(((bf16[16,128,512]{1,2,0:T(8,128)(2,1)}), bf16[16,128,512]{1,2,0:T(8,128)(2,1)S(1)}, u32[]{:S(2)}, u32[]{:S(2)}) %all-to-all-start.4) | async-done | bytes 2097184 | tf_op jit(solution)/shard_map/all_to_all | solution.py:59
  557.1 0.3 convert_reduce_fusion
  557.4 0.8 copy.72
  (41 shorter events, 0.5 us)
Async XLA Ops:
  7.2 2.1 copy-start.3
  7.2 123.6 %all-gather.11.cloned.1.call-start = ((), (), s32[]{:S(2)}) async-start(), calls=%async_computation.10 | async-start | bytes 9437184 | tf_op jit(solution)/shard_map/all_gather | solution.py:81
  7.9 222.4 %all-gather.9.cloned.1.call-start = ((), (), s32[]{:S(2)}) async-start(), calls=%async_computation.9 | async-start | bytes 17825792 | tf_op jit(solution)/shard_map/all_gather | solution.py:16
  9.2 2.5 copy-start
  10.4 286.8 %all-gather.7.cloned.1.call-start = ((), (), s32[]{:S(2)}) async-start(), calls=%async_computation.8 | async-start | bytes 2228224 | tf_op jit(solution)/shard_map/all_gather | solution.py:119
  11.1 332.8 %all-gather.5.cloned.1.call-start = ((), (), s32[]{:S(2)}) async-start(), calls=%async_computation.7 | async-start | bytes 4718592 | tf_op jit(solution)/shard_map/all_gather | solution.py:115
  11.7 2.6 copy-start.6
  246.4 26.5 %all-to-all-start.1 = ((f32[8,1,1024]{2,1,0:T(1,128)}), f32[8,1,1024]{2,1,0:T(1,128)S(1)}, u32[]{:S(2)}, u32[]{:S(2)}) async-start(f32[8,1,1024]{2,1,0:T(1,128)} %broadcast_in_dim.34), calls=%async_computation.1 | async-start | bytes 65536 | tf_op jit(solution)/shard_map/all_to_all | solution.py:26
  252.7 208.9 %reduce-scatter.2.cloned.1.call-start = ((), (), s32[]{:S(2)}) async-start(), calls=%async_computation.11 | async-start | bytes 9437184 | tf_op jit(solution)/shard_map/reduce_scatter | solution.py:101
  260.7 12.2 %copy-start.1 = (bf16[1024,1024]{0,1:T(8,128)(2,1)S(1)}, bf16[1024,1024]{0,1:T(8,128)(2,1)}, u32[]{:S(2)}) copy-start(bf16[1024,1024]{0,1:T(8,128)(2,1)} %copy.62) | copy-start | bytes 6291460
  288.4 0.8 copy-start.4
  288.4 1.0 copy-start.5
  289.4 7.1 %copy-start.2 = (bf16[1024,512]{1,0:T(8,128)(2,1)S(1)}, bf16[1024,512]{1,0:T(8,128)(2,1)}, u32[]{:S(2)}) copy-start(bf16[1024,512]{1,0:T(8,128)(2,1)} %param.16) | copy-start | bytes 3145732
  351.1 117.4 %all-to-all-start = ((f32[8,1,1024]{2,1,0:T(1,128)}), f32[8,1,1024]{2,1,0:T(1,128)S(1)}, u32[]{:S(2)}, u32[]{:S(2)}) async-start(f32[8,1,1024]{2,1,0:T(1,128)} %broadcast_in_dim.32), calls=%async_computation | async-start | bytes 65536 | tf_op jit(solution)/shard_map/all_to_all | solution.py:26
  467.2 7.2 %copy-start.7 = (bf16[512]{0:T(512)(128)(2,1)S(1)}, bf16[512]{0:T(512)(128)(2,1)}, u32[]{:S(2)}) copy-start(bf16[512]{0:T(512)(128)(2,1)} %param.19) | copy-start | bytes 3076
  468.4 22.8 %all-to-all-start.2 = ((bf16[16,64,513]{2,1,0:T(8,128)(2,1)}), bf16[16,64,513]{2,1,0:T(8,128)(2,1)S(1)}, u32[]{:S(2)}, u32[]{:S(2)}) async-start(bf16[16,64,513]{2,1,0:T(8,128)(2,1)} %pad_maximum_fusion), calls=%async_computation.3 | async-start | bytes 2621440 | tf_op jit(solution)/shard_map/all_to_all | solution.py:40
  508.4 14.5 %all-to-all-start.5 = ((f32[16,1,512]{2,1,0:T(1,128)}), f32[16,1,512]{2,1,0:T(1,128)S(1)}, u32[]{:S(2)}, u32[]{:S(2)}) async-start(f32[16,1,512]{2,1,0:T(1,128)} %broadcast_in_dim.63), calls=%async_computation.6 | async-start | bytes 65536 | tf_op jit(solution)/shard_map/all_to_all | solution.py:26
  523.0 34.1 %all-to-all-start.4 = ((bf16[16,128,512]{1,2,0:T(8,128)(2,1)}), bf16[16,128,512]{1,2,0:T(8,128)(2,1)S(1)}, u32[]{:S(2)}, u32[]{:S(2)}) async-start(bf16[16,128,512]{1,2,0:T(8,128)(2,1)} %bitcast.37), calls=%async_computation.5 | async-start | bytes 4194304 | tf_op jit(solution)/shard_map/all_to_all | solution.py:59
Sparse Core Ops, SparseCore 0:
  10.2 120.5 all-gather.10
  132.4 97.8 all-gather.8
  232.0 33.8 all-gather.6
  267.9 75.8 all-gather.4
  347.6 113.9 reduce-scatter.1
where the time goes:
time: 566 us; the launch traced here: 565 us
  waiting for transfers between devices  416 us (73%)
  local copies, waits for them, and re-layouts  44.6 us (8%)
  matrix products  42.8 us (8%)
  starting transfers between devices  29.1 us (5%)
  between operations  14 us (2%)
  blocking collectives  10.2 us (2%)
  other arithmetic  7.84 us (1%)
    all_gather x1, waiting for transfers between devices, shards(): attn_all = lax.all_gather(teacher_attn, 'teacher', axis=1, tiled=True)  117 us
    reduce_scatter x1, waiting for transfers between devices, shards(): lax.psum_scatter(jnp.einsum('tf,fko->kto', hidden, columns, preferred_ele...  107 us
    all_gather x1, waiting for transfers between devices, rows_first(): result, at, outs = (lax.all_gather(both, axis, axis=0, tiled=True), 0, [])  99.5 us
    all_gather x1, waiting for transfers between devices, shards(): attn_student = lax.all_gather(student_attn, 'teacher', axis=1, tiled=True)  46.7 us
    all_to_all x1, waiting for transfers between devices, sent_and_summed(): parts = lax.all_to_all(in_blocks(array, dim, peers), axis, 0, 0, tiled=True)  27.7 us
    transpose x2, local copies, waits for them, and re-layouts, rows_first(): outs.append(jnp.moveaxis(section, 0, dim))  20 us
    all_to_all x3, starting transfers between devices, sent_to_all(): lax.all_to_all(jnp.broadcast_to(array[None], (peers, *array.shape)), axis...  17 us
    all_to_all x1, waiting for transfers between devices, sent_together(): lax.all_to_all(both, axis, split_axis=split_dim, concat_axis=concat_dim,...  16.8 us
  transfers between devices with their start and end apart: 10, of which 6 were waited for; matrix products, arithmetic and copies ran while one was open for 15% of the time, Pallas kernels for 0%

commit v1 on v0

--- a/solution.py
+++ b/solution.py
@@ -112,7 +112,8 @@
     )
     target = moved.reshape(row_count, moved.shape[2])
     weight_mask = mask_got.reshape(row_count).astype(jnp.float32)
-    attn_student = lax.all_gather(student_attn, "teacher", axis=1, tiled=True)
+    blocks = lax.all_gather(student_attn, "teacher")
+    attn_student = jnp.concatenate(blocks, axis=1)
     columns = attn_student
     student_branch = jnp.dot(
         columns,

time: 566 us -> 560 us (0.989)
  waiting for transfers between devices: 416 us -> 401 us
  local copies, waits for them, and re-layouts: 44.6 us -> 50.7 us
    all_gather x1, waiting for transfers between devices: 46.7 us -> 6.93 us  [shards(): blocks = lax.all_gather(student_attn, 'teacher')]
    all_gather x1, waiting for transfers between devices: 0.02 us -> 27.4 us  [shards(): lax.all_gather(student_out_proj, 'student', axis=0, tiled=True)]
    reshape x0 -> x1, local copies, waits for them, and re-layouts: none -> 6.51 us  [shards(): attn_student = jnp.concatenate(blocks, axis=1)]
  transfers between devices with their start and end apart: 10 -> 10, of which waited for: 6 -> 7; matrix products, arithmetic and copies ran while one was open for 15% -> 17% of each run, Pallas kernels for 0% -> 0%
where the time goes in v1:
time: 560 us; the launch traced here: 559 us
  waiting for transfers between devices  401 us (72%)
  local copies, waits for them, and re-layouts  50.7 us (9%)
  matrix products  42.8 us (8%)
  starting transfers between devices  32 us (6%)
  between operations  14 us (2%)
  blocking collectives  10.2 us (2%)
  other arithmetic  7.84 us (1%)
    all_gather x1, waiting for transfers between devices, shards(): attn_all = lax.all_gather(teacher_attn, 'teacher', axis=1, tiled=True)  117 us
    reduce_scatter x1, waiting for transfers between devices, shards(): lax.psum_scatter(jnp.einsum('tf,fko->kto', hidden, columns, preferred_ele...  105 us
    all_gather x1, waiting for transfers between devices, rows_first(): result, at, outs = (lax.all_gather(both, axis, axis=0, tiled=True), 0, [])  99.5 us
    all_to_all x1, waiting for transfers between devices, sent_and_summed(): parts = lax.all_to_all(in_blocks(array, dim, peers), axis, 0, 0, tiled=True)  27.7 us
    all_gather x1, waiting for transfers between devices, shards(): lax.all_gather(student_out_proj, 'student', axis=0, tiled=True)  27.4 us
    all_to_all x3, starting transfers between devices, sent_to_all(): lax.all_to_all(jnp.broadcast_to(array[None], (peers, *array.shape)), axis...  19.9 us
    transpose x2, local copies, waits for them, and re-layouts, rows_first(): outs.append(jnp.moveaxis(section, 0, dim))  19.6 us
    all_to_all x1, waiting for transfers between devices, sent_together(): lax.all_to_all(both, axis, split_axis=split_dim, concat_axis=concat_dim,...  16.8 us
  transfers between devices with their start and end apart: 10, of which 7 were waited for; matrix products, arithmetic and copies ran while one was open for 17% of the time, Pallas kernels for 0%

profile of v1, /device:TPU:3, one launch (start us, length us, event | category | flops | bytes accessed | tf_op | source)
XLA Modules:
  0.0 558.9 jit_solution(8868351362170763385)
XLA Ops:
  7.2 0.7 all-gather.10.cloned.1.call-update
  8.0 1.2 copy.64
  9.2 1.1 pad_maximum_fusion.1
  10.4 0.7 all-gather.12.cloned.1.call-update
  11.1 0.5 all-gather.6.cloned.1.call-update
  11.7 2.6 copy.66
  14.3 116.5 %all-gather.10.cloned.1.call-done = bf16[1024,4096]{1,0:T(8,128)(2,1)} async-done(((bf16[1024,512]{1,0:T(8,128)(2,1)}), bf16[1024,4096]{1,0:T(8,128)(2,1)}) %all-gather.10.cloned.1.call-update) | async-done | bytes 8388624 | tf_op jit(solution)/shard_map/all_gather | solution.py:81
  130.8 99.5 %all-gather.8.cloned.1.call-done = bf16[4096,2048]{0,1:T(8,128)(2,1)} async-done(((bf16[256,2048]{0,1:T(8,128)(2,1)}), bf16[4096,2048]{0,1:T(8,128)(2,1)}) %all-gather.8.cloned.1.call-update) | async-done | bytes 16777232 | tf_op jit(solution)/shard_map/all_gather | solution.py:16
  230.3 15.4 %multiply_reduce_fusion = (f32[1024]{0:T(1024)S(1)}, f32[1024,1024]{1,0:T(8,128)}) fusion(bf16[1024,1024]{0,1:T(8,128)(2,1)} %copy.66, bf16[1024,4096]{1,0:T(8,128)(2,1)} %all-gather.10.cloned.1.call-done, bf16[4096,2048]{0,1:T(8,128)(2,1)} %all-gather.8.cloned.1.call-done), kind=kOutput, calls=%fused_computation.9 | convolution fusion | flops 8594127872 | bytes 23072768 | tf_op jit(solution)/shard_map/dot_general | solution.py:83
  245.8 0.6 broadcast_in_dim.34
  246.4 6.3 %all-to-all-start.1 = ((f32[8,1,1024]{2,1,0:T(1,128)}), f32[8,1,1024]{2,1,0:T(1,128)S(1)}, u32[]{:S(2)}, u32[]{:S(2)}) async-start(f32[8,1,1024]{2,1,0:T(1,128)} %broadcast_in_dim.34), calls=%async_computation.1 | async-start | bytes 65536 | tf_op jit(solution)/shard_map/all_to_all | solution.py:26
  252.7 0.2 reduce-scatter.2.cloned.1.call-start
  252.9 7.8 %slice_bitcast_fusion = bf16[1024,4096]{1,0:T(8,128)(2,1)} fusion(bf16[4096,2048]{0,1:T(8,128)(2,1)} %all-gather.8.cloned.1.call-done), kind=kLoop, calls=%fused_computation.4 | loop fusion | bytes 16777216 | tf_op jit(solution)/shard_map/transpose | solution.py:19
  260.7 11.8 %copy.65 = bf16[1024,4096]{0,1:T(8,128)(2,1)} copy(bf16[1024,4096]{1,0:T(8,128)(2,1)} %slice_bitcast_fusion) | data formatting | bytes 16777216 | tf_op jit(solution)/shard_map/transpose | solution.py:19
  272.6 15.4 %convert_bitcast_fusion = bf16[8,1024,512]{1,2,0:T(8,128)(2,1)} fusion(bf16[1024,8,512]{0,2,1:T(8,128)(2,1)} %bitcast.42, f32[1024,1024]{1,0:T(8,128)} %get-tuple-element.11, bf16[1024,1024]{0,1:T(8,128)(2,1)S(1)} %copy-done.1, f32[1024]{0:T(1024)S(1)} %convert_element_type.58, f32[1024]{0:T(1024)S(1)} %add_rsqrt_fusion), kind=kOutput, calls=%fused_computation.5 | convolution fusion | flops 8599371776 | bytes 23076864 | tf_op jit(solution)/shard_map/tf,fko->kto/dot_general | solution.py:102
  288.0 0.8 copy-done.4
  288.8 0.1 reshape.123
  289.1 6.8 %gather_fusion.1 = bf16[1024]{0:T(1024)(128)(2,1)S(1)} fusion(bf16[1024]{0:T(1024)(128)(2,1)S(1)} %select_convert_fusion, s32[1024]{0:T(1024)S(1)} %broadcast_clamp_fusion), kind=kCustom, calls=%fused_computation.1 | custom fusion | bytes 8192 | tf_op jit(solution)/shard_map/jit(_take)/gather | solution.py:99
  296.0 0.2 copy.70
  296.2 0.5 copy.61
  296.8 6.9 %all-gather.12.cloned.1.call-done = bf16[8192,256]{1,0:T(8,128)(2,1)} async-done(((bf16[1024,256]{1,0:T(8,128)(2,1)}), bf16[8192,256]{1,0:T(8,128)(2,1)}) %all-gather.12.cloned.1.call-update) | async-done | bytes 4194320 | tf_op jit(solution)/shard_map/all_gather | solution.py:115
  303.7 6.5 %copy.62 = bf16[1024,8,256]{0,2,1:T(8,128)(2,1)} copy(bf16[1024,8,256]{2,0,1:T(8,128)(2,1)} %bitcast.43) | data formatting | bytes 8388608 | tf_op jit(solution)/shard_map/reshape | solution.py:116
  310.2 27.4 %all-gather.6.cloned.1.call-done = bf16[2048,512]{1,0:T(8,128)(2,1)} async-done(((bf16[128,512]{1,0:T(8,128)(2,1)}), bf16[2048,512]{1,0:T(8,128)(2,1)}) %all-gather.6.cloned.1.call-update) | async-done | bytes 2097168 | tf_op jit(solution)/shard_map/all_gather | solution.py:120
  337.6 6.6 %multiply_reduce_fusion.3 = (f32[1024]{0:T(1024)S(1)}, f32[1024,512]{0,1:T(8,128)}) fusion(bf16[1024,2048]{0,1:T(8,128)(2,1)} %bitcast.44, bf16[2048,512]{1,0:T(8,128)(2,1)} %all-gather.6.cloned.1.call-done, bf16[1024,512]{0,1:T(8,128)(2,1)S(1)} %copy.61), kind=kOutput, calls=%fused_computation.19 | convolution fusion | flops 2149579776 | bytes 9441280 | tf_op jit(solution)/shard_map/dot_general | solution.py:118
  344.1 0.6 broadcast_in_dim.32
  344.8 6.1 %all-to-all-start = ((f32[8,1,1024]{2,1,0:T(1,128)}), f32[8,1,1024]{2,1,0:T(1,128)S(1)}, u32[]{:S(2)}, u32[]{:S(2)}) async-start(f32[8,1,1024]{2,1,0:T(1,128)} %broadcast_in_dim.32), calls=%async_computation | async-start | bytes 65536 | tf_op jit(solution)/shard_map/all_to_all | solution.py:26
  350.9 104.5 %reduce-scatter.2.cloned.1.call-done = bf16[1,1024,512]{1,2,0:T(8,128)(2,1)} async-done(((bf16[8,1024,512]{1,2,0:T(8,128)(2,1)}), bf16[1,1024,512]{1,2,0:T(8,128)(2,1)}) %reduce-scatter.2.cloned.1.call-update) | async-done | bytes 1048592 | tf_op jit(solution)/shard_map/reduce_scatter | solution.py:101
  455.4 1.5 copy.69
  456.9 4.0 gather_fusion
  460.9 0.2 broadcast_select_fusion
  461.1 1.2 pad_maximum_fusion
  462.3 6.0 %all-to-all-start.2 = ((bf16[16,64,513]{2,1,0:T(8,128)(2,1)}), bf16[16,64,513]{2,1,0:T(8,128)(2,1)S(1)}, u32[]{:S(2)}, u32[]{:S(2)}) async-start(bf16[16,64,513]{2,1,0:T(8,128)(2,1)} %pad_maximum_fusion), calls=%async_computation.3 | async-start | bytes 2621440 | tf_op jit(solution)/shard_map/all_to_all | solution.py:40
  468.4 16.8 %all-to-all-done.2 = bf16[16,64,513]{2,1,0:T(8,128)(2,1)S(1)} async-done(((bf16[16,64,513]{2,1,0:T(8,128)(2,1)}), bf16[16,64,513]{2,1,0:T(8,128)(2,1)S(1)}, u32[]{:S(2)}, u32[]{:S(2)}) %all-to-all-start.2) | async-done | bytes 1050656 | tf_op jit(solution)/shard_map/all_to_all | solution.py:40
  485.1 0.1 slice.22
  485.2 1.7 bitcast_convert_fusion
  486.9 1.9 copy.71
  488.8 0.2 multiply_reduce_fusion.4
  489.1 2.4 multiply_reduce_fusion.1
  491.5 10.2 %all_to_all.34 = f32[8,1,1024]{2,1,0:T(1,128)S(1)} all-to-all(f32[8,1,1024]{2,1,0:T(1,128)S(1)} %broadcast_in_dim.62), channel_id=1, replica_groups=mesh['teacher'=8,'student'=16] {'teacher'}, dimensions={0} | all-to-all | bytes 65536 | tf_op jit(solution)/shard_map/all_to_all | solution.py:26
  501.7 0.6 broadcast_in_dim.63
  502.4 7.5 %all-to-all-start.5 = ((f32[16,1,512]{2,1,0:T(1,128)}), f32[16,1,512]{2,1,0:T(1,128)S(1)}, u32[]{:S(2)}, u32[]{:S(2)}) async-start(f32[16,1,512]{2,1,0:T(1,128)} %broadcast_in_dim.63), calls=%async_computation.6 | async-start | bytes 65536 | tf_op jit(solution)/shard_map/all_to_all | solution.py:26
  509.9 5.4 fusion.6
  515.2 1.9 copy.86
  517.1 5.8 %all-to-all-start.4 = ((bf16[16,128,512]{1,2,0:T(8,128)(2,1)}), bf16[16,128,512]{1,2,0:T(8,128)(2,1)S(1)}, u32[]{:S(2)}, u32[]{:S(2)}) async-start(bf16[16,128,512]{1,2,0:T(8,128)(2,1)} %bitcast.41), calls=%async_computation.5 | async-start | bytes 4194304 | tf_op jit(solution)/shard_map/all_to_all | solution.py:59
  522.9 0.6 reduce_sum.89
  523.5 27.7 %all-to-all-done.4 = bf16[16,128,512]{1,2,0:T(8,128)(2,1)S(1)} async-done(((bf16[16,128,512]{1,2,0:T(8,128)(2,1)}), bf16[16,128,512]{1,2,0:T(8,128)(2,1)S(1)}, u32[]{:S(2)}, u32[]{:S(2)}) %all-to-all-start.4) | async-done | bytes 2097184 | tf_op jit(solution)/shard_map/all_to_all | solution.py:59
  551.2 0.3 convert_reduce_fusion
  551.5 0.8 copy.76
  (42 shorter events, 0.6 us)
Async XLA Ops:
  7.2 2.1 copy-start.3
  7.2 123.6 %all-gather.10.cloned.1.call-start = ((), (), s32[]{:S(2)}) async-start(), calls=%async_computation.9 | async-start | bytes 9437184 | tf_op jit(solution)/shard_map/all_gather | solution.py:81
  7.9 222.4 %all-gather.8.cloned.1.call-start = ((), (), s32[]{:S(2)}) async-start(), calls=%async_computation.8 | async-start | bytes 17825792 | tf_op jit(solution)/shard_map/all_gather | solution.py:16
  9.2 2.5 copy-start
  10.4 293.3 %all-gather.12.cloned.1.call-start = ((), (), s32[]{:S(2)}) async-start(), calls=%async_computation.11 | async-start | bytes 4718592 | tf_op jit(solution)/shard_map/all_gather | solution.py:115
  11.1 326.5 %all-gather.6.cloned.1.call-start = ((), (), s32[]{:S(2)}) async-start(), calls=%async_computation.7 | async-start | bytes 2228224 | tf_op jit(solution)/shard_map/all_gather | solution.py:120
  11.7 2.6 copy-start.6
  246.4 26.1 %all-to-all-start.1 = ((f32[8,1,1024]{2,1,0:T(1,128)}), f32[8,1,1024]{2,1,0:T(1,128)S(1)}, u32[]{:S(2)}, u32[]{:S(2)}) async-start(f32[8,1,1024]{2,1,0:T(1,128)} %broadcast_in_dim.34), calls=%async_computation.1 | async-start | bytes 65536 | tf_op jit(solution)/shard_map/all_to_all | solution.py:26
  252.7 202.7 %reduce-scatter.2.cloned.1.call-start = ((), (), s32[]{:S(2)}) async-start(), calls=%async_computation.10 | async-start | bytes 9437184 | tf_op jit(solution)/shard_map/reduce_scatter | solution.py:101
  260.7 11.9 %copy-start.1 = (bf16[1024,1024]{0,1:T(8,128)(2,1)S(1)}, bf16[1024,1024]{0,1:T(8,128)(2,1)}, u32[]{:S(2)}) copy-start(bf16[1024,1024]{0,1:T(8,128)(2,1)} %copy.66) | copy-start | bytes 6291460
  288.0 0.8 copy-start.4
  288.0 1.0 copy-start.5
  289.1 7.1 %copy-start.2 = (bf16[1024,512]{1,0:T(8,128)(2,1)S(1)}, bf16[1024,512]{1,0:T(8,128)(2,1)}, u32[]{:S(2)}) copy-start(bf16[1024,512]{1,0:T(8,128)(2,1)} %param.16) | copy-start | bytes 3145732
  344.8 117.6 %all-to-all-start = ((f32[8,1,1024]{2,1,0:T(1,128)}), f32[8,1,1024]{2,1,0:T(1,128)S(1)}, u32[]{:S(2)}, u32[]{:S(2)}) async-start(f32[8,1,1024]{2,1,0:T(1,128)} %broadcast_in_dim.32), calls=%async_computation | async-start | bytes 65536 | tf_op jit(solution)/shard_map/all_to_all | solution.py:26
  461.1 7.2 %copy-start.7 = (bf16[512]{0:T(512)(128)(2,1)S(1)}, bf16[512]{0:T(512)(128)(2,1)}, u32[]{:S(2)}) copy-start(bf16[512]{0:T(512)(128)(2,1)} %param.19) | copy-start | bytes 3076
  462.3 22.8 %all-to-all-start.2 = ((bf16[16,64,513]{2,1,0:T(8,128)(2,1)}), bf16[16,64,513]{2,1,0:T(8,128)(2,1)S(1)}, u32[]{:S(2)}, u32[]{:S(2)}) async-start(bf16[16,64,513]{2,1,0:T(8,128)(2,1)} %pad_maximum_fusion), calls=%async_computation.3 | async-start | bytes 2621440 | tf_op jit(solution)/shard_map/all_to_all | solution.py:40
  502.4 14.7 %all-to-all-start.5 = ((f32[16,1,512]{2,1,0:T(1,128)}), f32[16,1,512]{2,1,0:T(1,128)S(1)}, u32[]{:S(2)}, u32[]{:S(2)}) async-start(f32[16,1,512]{2,1,0:T(1,128)} %broadcast_in_dim.63), calls=%async_computation.6 | async-start | bytes 65536 | tf_op jit(solution)/shard_map/all_to_all | solution.py:26
  517.1 34.1 %all-to-all-start.4 = ((bf16[16,128,512]{1,2,0:T(8,128)(2,1)}), bf16[16,128,512]{1,2,0:T(8,128)(2,1)S(1)}, u32[]{:S(2)}, u32[]{:S(2)}) async-start(bf16[16,128,512]{1,2,0:T(8,128)(2,1)} %bitcast.41), calls=%async_computation.5 | async-start | bytes 4194304 | tf_op jit(solution)/shard_map/all_to_all | solution.py:59
Sparse Core Ops, SparseCore 0:
  10.2 120.5 all-gather.9
  132.4 97.8 all-gather.7
  232.7 70.9 all-gather.11
  305.3 32.2 all-gather.5
  341.3 114.1 reduce-scatter.1
